TPU v7x, 8 devices: a whole 2x2x1 slice. The times are simulated.
8 devices in a mesh: dp: 1 (over z), depth: 2 (over y), col: 2 (over x), row: 2 (over core).
Axes of the slice: x: 2, y: 2, z: 1, core: 2. Of those that a mesh axis runs over, the one named last changes fastest.
Arguments:
- x_in: bfloat16 [16384, 2048], P(('dp', 'depth', 'row'), 'col')
- ln_gamma: float32 [2048], P('col')
- ln_beta: float32 [2048], P('col')
- w_up: bfloat16 [2048, 8192], P('row', 'col')
- b_up: bfloat16 [8192], P('col')
- w_down: bfloat16 [8192, 2048], P('row', 'col')
- b_down: bfloat16 [2048], P('col')
- grad_out: bfloat16 [16384, 2048], P(('dp', 'depth', 'row'), 'col')
Outputs:
- output 1: bfloat16 [16384, 2048], P(('dp', 'depth', 'row'), 'col')
- output 2: bfloat16 [16384, 2048], P(('dp', 'depth', 'row'), 'col')
- output 3: float32 [2048], P(('dp', 'col'))
- output 4: float32 [2048], P(('dp', 'col'))
- output 5: bfloat16 [2048, 8192], P(('dp', 'row'), 'col')
- output 6: float32 [8192], P(('dp', 'col'))
- output 7: bfloat16 [8192, 2048], P(('dp', 'row'), 'col')
- output 8: float32 [2048], P(('dp', 'col'))
All inputs are finite; a program needn't handle non-finite values.
Results may differ from a plain program's by a relative error of at most 0.0111574.
Values are sent between devices in bfloat16 or wider.
A program may use at most 1 GiB of HBM per device.

v0:
```python
import jax
import jax.numpy as jnp
from jax import lax
from jax.sharding import PartitionSpec as P

LN_EPS = 1e-5


def gelu_tanh(values):
    return jax.nn.gelu(values, approximate=True)


def solution(mesh):
    col_size = mesh.shape['col']
    token_axes = ('depth', 'row')
    tok_spec = P(('dp', 'depth', 'row'), 'col')
    vec_spec = P('col')
    mat_spec = P('row', 'col')
    grad_vec = P(('dp', 'col'))
    grad_mat = P(('dp', 'row'), 'col')

    def local_pass(x_blk, gamma_blk, beta_blk, w_up_blk, b_up_blk, w_down_blk, b_down_blk, dy_blk):
        inv_width = 1.0 / (x_blk.shape[1] * col_size)
        x_f32 = x_blk.astype(jnp.float32)
        row_mean = lax.psum(jnp.sum(x_f32, axis=1, keepdims=True), 'col') * inv_width
        centered = x_f32 - row_mean
        row_var = lax.psum(jnp.sum(centered * centered, axis=1, keepdims=True), 'col') * inv_width
        inv_std = lax.rsqrt(row_var + LN_EPS)
        x_hat = centered * inv_std
        x_norm = (x_hat * gamma_blk + beta_blk).astype(jnp.bfloat16)
        norm_rows = lax.all_gather(x_norm, 'col', axis=1, tiled=True)
        w_up_cols = lax.all_gather(w_up_blk, 'row', axis=0, tiled=True)
        pre_act = (jnp.dot(norm_rows, w_up_cols, preferred_element_type=jnp.float32) + b_up_blk.astype(jnp.float32)).astype(jnp.bfloat16)
        act_f32, gelu_vjp = jax.vjp(gelu_tanh, pre_act.astype(jnp.float32))
        hidden = act_f32.astype(jnp.bfloat16)
        hidden_rows = lax.all_gather(hidden, 'col', axis=1, tiled=True)
        w_down_cols = lax.all_gather(w_down_blk, 'row', axis=0, tiled=True)
        y_blk = (x_f32 + jnp.dot(hidden_rows, w_down_cols, preferred_element_type=jnp.float32) + b_down_blk.astype(jnp.float32)).astype(jnp.bfloat16)
        dy_f32 = dy_blk.astype(jnp.float32)
        grad_b_down = lax.psum(jnp.sum(dy_f32, axis=0), token_axes)
        down_part = jnp.einsum('tf,th->fh', hidden_rows, dy_blk, preferred_element_type=jnp.float32)
        grad_w_down = lax.psum(lax.psum_scatter(down_part, 'row', scatter_dimension=0, tiled=True), 'depth').astype(jnp.bfloat16)
        hidden_part = jnp.einsum('th,fh->tf', dy_blk, w_down_cols, preferred_element_type=jnp.float32)
        grad_hidden = lax.psum_scatter(hidden_part, 'col', scatter_dimension=1, tiled=True)
        grad_pre = gelu_vjp(grad_hidden)[0].astype(jnp.bfloat16)
        grad_b_up = lax.psum(jnp.sum(grad_pre.astype(jnp.float32), axis=0), token_axes)
        up_part = jnp.einsum('th,tf->hf', norm_rows, grad_pre, preferred_element_type=jnp.float32)
        grad_w_up = lax.psum(lax.psum_scatter(up_part, 'row', scatter_dimension=0, tiled=True), 'depth').astype(jnp.bfloat16)
        norm_part = jnp.einsum('tf,hf->th', grad_pre, w_up_cols, preferred_element_type=jnp.float32)
        grad_norm = lax.psum_scatter(norm_part, 'col', scatter_dimension=1, tiled=True)
        grad_gamma = lax.psum(jnp.sum(grad_norm * x_hat, axis=0), token_axes)
        grad_beta = lax.psum(jnp.sum(grad_norm, axis=0), token_axes)
        grad_hat = grad_norm * gamma_blk
        sum_plain, sum_proj = lax.psum((jnp.sum(grad_hat, axis=1, keepdims=True), jnp.sum(grad_hat * x_hat, axis=1, keepdims=True)), 'col')
        grad_x = (dy_f32 + inv_std * (grad_hat - sum_plain * inv_width - x_hat * (sum_proj * inv_width))).astype(jnp.bfloat16)
        return y_blk, grad_x, grad_gamma, grad_beta, grad_w_up, grad_b_up, grad_w_down, grad_b_down

    return jax.shard_map(
        local_pass,
        mesh=mesh,
        in_specs=(tok_spec, vec_spec, vec_spec, mat_spec, vec_spec, mat_spec, vec_spec, tok_spec),
        out_specs=(tok_spec, tok_spec, grad_vec, grad_vec, grad_mat, grad_vec, grad_mat, grad_vec),
        check_vma=False,
    )
```

profile of v0, /device:TPU:0, one launch (start us, length us, event | category | flops | bytes accessed | tf_op | source)
XLA Modules:
  0.0 3915.7 jit_solution(2494237663946229135)
XLA Ops:
  7.2 0.7 all-gather.11.cloned.1.call-update
  8.0 4.5 convert_reduce_fusion.1
  12.5 10.1 psum.70
  22.6 5.4 fusion.22
  28.0 6.7 psum.71
  35.4 8.5 fusion.17
  44.0 0.7 all-gather.7.cloned.1.call-update
  44.9 81.4 %fusion.27 = f32[4096,8192]{1,0:T(8,128)} fusion(bf16[4096,1024]{1,0:T(8,128)(2,1)} %param.15, bf16[8192,1024]{1,0:T(8,128)(2,1)} %all-gather.11.cloned.1.call-done), kind=kOutput, calls=%fused_computation.43 | convolution fusion | flops 68719476736 | bytes 159383552 | tf_op jit(solution)/shard_map/th,fh->tf/dot_general | solution.py:43
  127.0 115.2 %all-gather.5.cloned.1.call-done = bf16[4096,2048]{1,0:T(8,128)(2,1)} async-done(((bf16[4096,1024]{1,0:T(8,128)(2,1)}), bf16[4096,2048]{1,0:T(8,128)(2,1)}) %all-gather.5.cloned.1.call-update) | async-done | bytes 16777232 | tf_op jit(solution)/shard_map/all_gather | solution.py:31
  242.2 29.4 all-gather.7.cloned.1.call-done
  271.5 1448.0 %reduce-scatter.5.cloned.1.call-done = f32[4096,4096]{1,0:T(8,128)} async-done(((f32[4096,8192]{1,0:T(8,128)}), f32[4096,4096]{1,0:T(8,128)}) %reduce-scatter.5.cloned.1.call-update) | async-done | bytes 67108880 | tf_op jit(solution)/shard_map/reduce_scatter | solution.py:44
  1719.5 129.1 %convert_reduce_fusion = (f32[4096]{0:T(1024)}, bf16[4096,4096]{1,0:T(8,128)(2,1)}, bf16[4096,4096]{1,0:T(8,128)(2,1)}) fusion(f32[4096,4096]{1,0:T(8,128)} %reduce-scatter.5.cloned.1.call-done, f32[4096]{0:T(1024)S(1)} %convert_element_type.44, bf16[4096,2048]{1,0:T(8,128)(2,1)} %all-gather.5.cloned.1.call-done, ...), kind=kOutput, calls=%fused_computation.15 | convolution fusion | flops 69172461568 | bytes 167804928 | tf_op jit(solution)/shard_map/dot_general | solution.py:33
  1849.0 79.3 %fusion.29 = f32[2048,4096]{1,0:T(8,128)} fusion(bf16[4096,2048]{1,0:T(8,128)(2,1)} %all-gather.5.cloned.1.call-done, bf16[4096,4096]{1,0:T(8,128)(2,1)} %get-tuple-element.21), kind=kOutput, calls=%fused_computation.45 | convolution fusion | flops 68719476736 | bytes 83886080 | tf_op jit(solution)/shard_map/th,tf->hf/dot_general | solution.py:47
  1928.9 78.6 %fusion.28 = f32[4096,2048]{1,0:T(8,128)} fusion(bf16[4096,4096]{1,0:T(8,128)(2,1)} %get-tuple-element.21, bf16[2048,4096]{1,0:T(8,128)(2,1)} %all-gather.7.cloned.1.call-done), kind=kOutput, calls=%fused_computation.44 | convolution fusion | flops 68719476736 | bytes 83886080 | tf_op jit(solution)/shard_map/tf,hf->th/dot_general | solution.py:49
  2007.7 604.3 %all-gather.9.cloned.1.call-done = bf16[4096,8192]{1,0:T(8,128)(2,1)} async-done(((bf16[4096,4096]{1,0:T(8,128)(2,1)}), bf16[4096,8192]{1,0:T(8,128)(2,1)}) %all-gather.9.cloned.1.call-update) | async-done | bytes 67108880 | tf_op jit(solution)/shard_map/all_gather | solution.py:36
  2612.0 79.3 %fusion.30 = f32[8192,1024]{1,0:T(8,128)} fusion(bf16[4096,8192]{1,0:T(8,128)(2,1)} %all-gather.9.cloned.1.call-done, bf16[4096,1024]{1,0:T(8,128)(2,1)} %param.15), kind=kOutput, calls=%fused_computation.46 | convolution fusion | flops 68719476736 | bytes 109051904 | tf_op jit(solution)/shard_map/tf,th->fh/dot_general | solution.py:41
  2691.3 0.6 copy-done.9
  2692.0 330.9 %reduce-scatter.7.cloned.1.call-done = f32[4096,1024]{1,0:T(8,128)} async-done(((f32[4096,2048]{1,0:T(8,128)}), f32[4096,1024]{1,0:T(8,128)}) %reduce-scatter.7.cloned.1.call-update) | async-done | bytes 16777232 | tf_op jit(solution)/shard_map/reduce_scatter | solution.py:50
  3022.9 11.0 fusion.21
  3033.9 7.4 all-reduce.1
  3041.4 16.2 convert_reduce_fusion.2
  3057.6 10.9 all-reduce
  3068.4 80.0 %fusion.25 = bf16[4096,1024]{1,0:T(8,128)(2,1)} fusion(bf16[4096,1024]{1,0:T(8,128)(2,1)} %param.8, bf16[4096,8192]{1,0:T(8,128)(2,1)} %all-gather.9.cloned.1.call-done, bf16[8192,1024]{1,0:T(8,128)(2,1)} %all-gather.11.cloned.1.call-done, f32[1024]{0:T(1024)S(1)} %convert_element_type.48), kind=kOutput, calls=%fused_computation.37 | convolution fusion | flops 68736253952 | bytes 100667392 | tf_op jit(solution)/shard_map/dot_general | solution.py:38
  3148.5 760.1 %all-reduce.4 = (bf16[1024,4096]{1,0:T(8,128)(2,1)}, bf16[4096,1024]{1,0:T(8,128)(2,1)}) all-reduce(f32[1024,4096]{1,0:T(8,128)} %reduce-scatter.9.cloned.1.call-done, f32[4096,1024]{1,0:T(8,128)} %reduce-scatter.11.cloned.1.call-done), channel_id=1, replica_groups=mesh['dp'=1,'depth'=2,'col'=2,'row'=2] {'depth'}, use_global_device_ids=true, to_apply=%region_15.0 | all-reduce | flops 8388608 | bytes 50331648 | tf_op jit(solution)/shard_map/psum | solution.py:48
  (41 shorter events, 2.8 us)
Async XLA Ops:
  7.2 28.2 copy-start.8
  7.2 28.2 copy-start.4
  7.2 37.7 all-gather.11.cloned.1.call-start
  7.9 234.2 %all-gather.5.cloned.1.call-start = ((), (), s32[]{:S(2)}) async-start(), calls=%async_computation.4 | async-start | bytes 25165824 | tf_op jit(solution)/shard_map/all_gather | solution.py:31
  22.6 21.3 copy-start
  34.8 0.6 copy-start.2
  43.9 227.6 %all-gather.7.cloned.1.call-start = ((), (), s32[]{:S(2)}) async-start(), calls=%async_computation.5 | async-start | bytes 25165824 | tf_op jit(solution)/shard_map/all_gather | solution.py:32
  44.7 1674.9 %reduce-scatter.5.cloned.1.call-start = ((), (), s32[]{:S(2)}) async-start(), calls=%async_computation.8 | async-start | bytes 201326592 | tf_op jit(solution)/shard_map/reduce_scatter | solution.py:44
  126.3 0.7 copy-start.7
  126.3 2485.7 %all-gather.9.cloned.1.call-start = ((), (), s32[]{:S(2)}) async-start(), calls=%async_computation.6 | async-start | bytes 100663296 | tf_op jit(solution)/shard_map/all_gather | solution.py:36
  1848.7 843.3 %reduce-scatter.9.cloned.1.call-start = ((), (), s32[]{:S(2)}) async-start(), calls=%async_computation.10 | async-start | bytes 50331648 | tf_op jit(solution)/shard_map/reduce_scatter | solution.py:48
  1928.3 1094.5 %reduce-scatter.7.cloned.1.call-start = ((), (), s32[]{:S(2)}) async-start(), calls=%async_computation.9 | async-start | bytes 50331648 | tf_op jit(solution)/shard_map/reduce_scatter | solution.py:50
  2007.5 1141.0 %reduce-scatter.11.cloned.1.call-start = ((), (), s32[]{:S(2)}) async-start(), calls=%async_computation.11 | async-start | bytes 50331648 | tf_op jit(solution)/shard_map/reduce_scatter | solution.py:42
  2691.3 0.7 copy-start.9
  2691.3 331.6 %copy-start.1 = (f32[4096,1]{0,1:T(1,128)S(1)}, f32[4096,1]{0,1:T(1,128)}, u32[]{:S(2)}) copy-start(f32[4096,1]{0,1:T(1,128)} %copy-done) | copy-start | bytes 49156
  2691.3 331.6 %copy-start.3 = (f32[4096,1]{0,1:T(1,128)S(1)}, f32[4096,1]{0,1:T(1,128)}, u32[]{:S(2)}) copy-start(f32[4096,1]{0,1:T(1,128)} %copy-done.2) | copy-start | bytes 49156
  2691.3 331.6 %copy-start.5 = (f32[1024]{0:T(1024)S(1)}, f32[1024]{0:T(1024)}, u32[]{:S(2)}) copy-start(f32[1024]{0:T(1024)} %param.9) | copy-start | bytes 12292
  3041.4 16.2 copy-start.6
Sparse Core Ops, SparseCore 0:
  9.5 30.6 all-gather.10
  44.0 198.0 all-gather.4
  243.7 27.8 all-gather.6
  273.6 1445.8 reduce-scatter.4
  1848.8 763.1 all-gather.8
  2614.1 39.1 reduce-scatter.8
  2655.6 367.2 reduce-scatter.6
  3025.1 39.1 reduce-scatter.10
where the time goes:
time: 3920 us
  waiting for transfers between devices  2530 us (65%)
  blocking collectives  795 us (20%)
  matrix products  528 us (13%)
  other arithmetic  45.8 us (1%)
    reduce_scatter x1, waiting for transfers between devices, local_pass(): lax.psum_scatter(hidden_part, 'col', scatter_dimension=1, tiled=True)  1450 us
    psum x1, blocking collectives, local_pass(): lax.psum(lax.psum_scatter(up_part, 'row', scatter_dimension=0, tiled=True...  760 us
    all_gather x1, waiting for transfers between devices, local_pass(): hidden_rows = lax.all_gather(hidden, 'col', axis=1, tiled=True)  604 us
    reduce_scatter x1, waiting for transfers between devices, local_pass(): lax.psum_scatter(norm_part, 'col', scatter_dimension=1, tiled=True)  331 us
    dot_general x1, matrix products, local_pass(): jnp.dot(norm_rows, w_up_cols, preferred_element_type=jnp.float32)  129 us
    all_gather x1, waiting for transfers between devices, local_pass(): norm_rows = lax.all_gather(x_norm, 'col', axis=1, tiled=True)  115 us
    dot_general x1, matrix products, local_pass(): jnp.einsum('th,fh->tf', dy_blk, w_down_cols, preferred_element_type=jnp.f...  81.4 us
    dot_general x1, matrix products, local_pass(): jnp.dot(hidden_rows, w_down_cols, preferred_element_type=jnp.float32)  80 us
  transfers between devices with their start and end apart: 8, of which 5 were waited for; matrix products, arithmetic and copies ran while one was open for 11% of the time, Pallas kernels for 0%

commit v1 on v0

v1 whole, which is shorter than its diff:
```python
import jax
import jax.numpy as jnp
from jax import lax
from jax.sharding import PartitionSpec as P


LN_EPS = 1e-5
F32 = jnp.float32
BF16 = jnp.bfloat16
GELU_A = 0.7978845608028654
GELU_B = 0.044715


def gelu_value(v):
    return 0.5 * v * (1.0 + jnp.tanh(GELU_A * (v + GELU_B * (v * v * v))))


def gelu_slope(v):
    sq = v * v
    t = jnp.tanh(GELU_A * (v + GELU_B * (v * sq)))
    return 0.5 * (1.0 + t) + (0.5 * v) * (1.0 - t * t) * (GELU_A + (3.0 * GELU_A * GELU_B) * sq)


def mm(a, b, dims):
    return lax.dot_general(a, b, (dims, ((), ())), preferred_element_type=F32)


NN = ((1,), (0,))
NT = ((1,), (1,))
TN = ((0,), (0,))


def pick(flag, a, b):
    return jnp.where(flag, a, b)


def solution(mesh):
    tok_spec = P(('dp', 'depth', 'row'), 'col')
    vec_spec = P('col')
    mat_spec = P('row', 'col')
    grad_vec = P(('dp', 'col'))
    grad_mat = P(('dp', 'row'), 'col')
    swap = [(0, 1), (1, 0)]

    def local_pass(x, gamma, beta, w_up, b_up, w_down, b_down, dy):
        c = lax.axis_index('col')
        r = lax.axis_index('row')
        d = lax.axis_index('depth')
        rows, half = x.shape
        own = rows // 2
        width = half * 2
        ffn = w_down.shape[0]

        def hop(axis, value, pairs=swap):
            return lax.ppermute(value, axis, pairs)

        def rows_of(value, which, size):
            return lax.dynamic_slice_in_dim(value, which * size, size, 0)

        def cols_of(value, which, size):
            return lax.dynamic_slice_in_dim(value, which * size, size, 1)

        def after(value, *deps):
            return lax.optimization_barrier((value,) + deps)[0]

        def placed(out, axis, parts):
            for index, value in parts:
                out = lax.dynamic_update_slice_in_dim(out, value, index * value.shape[axis], axis)
            return out

        small = jnp.concatenate([gamma, beta, b_up.astype(F32), b_down.astype(F32)])
        small = lax.all_gather(small, 'col', axis=0, tiled=False)
        x, dy, w_up, w_down, small = lax.optimization_barrier((x, dy, w_up, w_down, small))
        peer_vec = lax.dynamic_index_in_dim(small, 1 - c, 0, keepdims=False)
        gam_peer, bet_peer = peer_vec[:half], peer_vec[half:width]
        b_oth = peer_vec[width:width + ffn]
        bd_mine, bd_peer = b_down.astype(F32), peer_vec[width + ffn:]

        x_peer = hop('col', x)
        diag = r == c
        quarter = ffn // 4
        lent = hop(('col', 'row'), rows_of(w_down, (1 - r) * 2 + d, quarter), [(1, 0), (2, 3)])
        d_got = hop('col', pick(diag, lent, rows_of(w_down, r * 2 + d, quarter)))
        dy_peer = hop('col', dy)
        u_got = hop('col', w_up)
        d_rest = hop(('col', 'row'), w_down, [(0, 2), (3, 1)])

        def own_rows(v):
            return rows_of(v, c, own)

        d_mine = lax.all_gather(w_down, 'row', axis=0, tiled=True)
        w_up_c = lax.all_gather(w_up, 'row', axis=0, tiled=True)
        d_peer = lax.all_gather(d_got, ('row', 'depth'), axis=0, tiled=True)
        d_far = lax.all_gather(d_rest, 'row', axis=0, tiled=True)
        w_up_o = lax.all_gather(u_got, 'row', axis=0, tiled=True)
        dm_c, dm_o = rows_of(d_mine, c, ffn), rows_of(d_mine, 1 - c, ffn)
        dp_c, dp_o = d_peer, rows_of(d_far, 1 - c, ffn)

        da_c = lax.optimization_barrier(mm(dy, dm_c, NT))
        da_o = lax.optimization_barrier(mm(own_rows(after(dy, da_c)), dm_o, NT))
        dbd = jnp.sum(dy.astype(F32), axis=0)
        inv_width = 1.0 / width
        sum_mine = lax.optimization_barrier(jnp.sum(x.astype(F32), axis=1, keepdims=True))
        x_peer = after(x_peer, da_o, dbd)
        mu = (sum_mine + jnp.sum(x_peer.astype(F32), axis=1, keepdims=True)) * inv_width

        def square_sum(v):
            cen = v.astype(F32) - mu
            return jnp.sum(cen * cen, axis=1, keepdims=True)

        var = (square_sum(x) + square_sum(x_peer)) * inv_width
        mu, inv = lax.optimization_barrier((mu, lax.rsqrt(var + LN_EPS)))

        def normed(v, g, b):
            return (((v.astype(F32) - mu) * inv) * g + b).astype(BF16)

        xn = placed(jnp.zeros((rows, width), BF16), 1, [(c, normed(x, gamma, beta)), (1 - c, normed(x_peer, gam_peer, bet_peer))])
        xn = after(xn, da_o)

        u_c = (mm(xn, w_up_c, NN) + b_up.astype(F32)).astype(BF16)
        a_c = gelu_value(u_c.astype(F32)).astype(BF16)

        f2, f4 = ffn // 2, ffn // 4
        give = lax.optimization_barrier(mm(cols_of(a_c, 1 - r, f2), dy, TN))
        got = hop('row', give)
        ym_c = lax.optimization_barrier(mm(own_rows(after(a_c, give)), dm_c, NN))
        s = lax.optimization_barrier(mm(cols_of(after(a_c, ym_c), r, f2), dy, TN) + got)
        m_d = lax.optimization_barrier((rows_of(s, d, f4) + hop('depth', rows_of(s, 1 - d, f4))).astype(BF16))

        da_c = da_c + mm(after(dy_peer, s), dp_c, NT)
        du_c = (da_c * gelu_slope(u_c.astype(F32))).astype(BF16)
        dbu = jnp.sum(du_c.astype(F32), axis=0)
        du_c, dbu = lax.optimization_barrier((du_c, dbu))
        m_e = hop('depth', m_d)
        m_got = hop(('col', 'row'), jnp.stack([m_d, m_e]), [(1, 0), (2, 3)])

        e = width // 4
        give = lax.optimization_barrier(mm(cols_of(after(a_c, du_c), 1 - r, f2), dy_peer, TN))
        got = hop('row', give)
        q1 = lax.optimization_barrier(mm(cols_of(after(xn, give), (1 - r) * 2 + (1 - d), e), du_c, TN))
        g1 = hop('row', q1)
        s = lax.optimization_barrier(mm(cols_of(after(a_c, q1), r, f2), dy_peer, TN) + got)
        n_d = lax.optimization_barrier((rows_of(s, d, f4) + hop('depth', rows_of(s, 1 - d, f4))).astype(BF16))
        q2 = lax.optimization_barrier(mm(cols_of(after(xn, s), (1 - r) * 2 + d, e), du_c, TN))
        g2 = hop('row', q2)
        q3 = lax.optimization_barrier(mm(cols_of(after(xn, q2), r * 2 + (1 - d), e), du_c, TN) + g1)
        got = hop('depth', q3)
        q4 = lax.optimization_barrier(mm(cols_of(after(xn, q3), r * 2 + d, e), du_c, TN) + g2)
        dwu_d = lax.optimization_barrier((q4 + got).astype(BF16))
        dwu_e = hop('depth', dwu_d)
        dwu = placed(lax.optimization_barrier(placed(jnp.zeros((half, ffn), BF16), 0, [(d, dwu_d)])), 0, [(1 - d, dwu_e)])

        n_a = hop(('col', 'row'), n_d, [(0, 2), (3, 1)])
        n_b = hop(('col', 'row'), n_d, [(1, 2), (2, 1)])
        n_got = hop(('depth', 'col', 'row'), jnp.stack([n_a, n_b]), [(1, 5), (5, 1), (2, 6), (6, 2)])
        dxn_c = lax.optimization_barrier(mm(own_rows(after(du_c, q4)), w_up_c, NT))
        yp_c = lax.optimization_barrier(mm(own_rows(after(a_c, dxn_c)), dp_c, NN))

        u_o = (mm(own_rows(after(xn, yp_c)), w_up_o, NN) + b_oth).astype(BF16)
        a_o = gelu_value(u_o.astype(F32)).astype(BF16)
        x_own, xr_own = own_rows(x), own_rows(x_peer)
        dy_own, dyr_own = own_rows(dy), own_rows(dy_peer)
        y_give = ((xr_own.astype(F32) + (yp_c + mm(a_o, dp_o, NN))) + bd_peer).astype(BF16)
        y_give = lax.optimization_barrier(y_give)
        y_got = hop('col', y_give)

        da_o = da_o + mm(own_rows(after(dy_peer, y_give)), dp_o, NT)
        du_o = (da_o * gelu_slope(u_o.astype(F32))).astype(BF16)
        du_o = lax.optimization_barrier(du_o)

        mu_o, inv_o = own_rows(mu), own_rows(inv)
        dx_gives, dx_keeps, sums_k = [], [], []
        parts = 2
        n = own // parts
        prev = du_o
        for k in range(parts):
            cut = slice(k * n, (k + 1) * n)
            dxn = dxn_c[cut] + mm(after(du_o, prev)[cut], w_up_o, NT)
            dxn = lax.optimization_barrier(dxn)
            mk, ik = mu_o[cut], inv_o[cut]
            near, far = cols_of(dxn, c, half), cols_of(dxn, 1 - c, half)
            h_near = (x_own[cut].astype(F32) - mk) * ik
            h_far = (xr_own[cut].astype(F32) - mk) * ik
            g_near, g_far = near * gamma, far * gam_peer
            mg = (jnp.sum(g_near, 1, keepdims=True) + jnp.sum(g_far, 1, keepdims=True)) * inv_width
            mp = (jnp.sum(g_near * h_near, 1, keepdims=True) + jnp.sum(g_far * h_far, 1, keepdims=True)) * inv_width
            sums_k.append([jnp.sum(near * h_near, 0), jnp.sum(far * h_far, 0), jnp.sum(near, 0), jnp.sum(far, 0)])
            mg, mp = lax.optimization_barrier((mg, mp))
            dx_far = (dyr_own[cut].astype(F32) + ik * (g_far - mg - h_far * mp)).astype(BF16)
            prev = dx_far = lax.optimization_barrier(dx_far)
            dx_gives.append(hop('col', dx_far))
            dx_keeps.append((dy_own[cut].astype(F32) + ik * (g_near - mg - h_near * mp)).astype(BF16))

        a_l = after(a_o, prev)
        y_keep = ((x_own.astype(F32) + (ym_c + mm(a_l, dm_o, NN))) + bd_mine).astype(BF16)
        y_keep = lax.optimization_barrier(y_keep)
        y_out = lax.optimization_barrier(placed(jnp.zeros((rows, half), BF16), 0, [(c, y_keep), (1 - c, y_got)]))
        dx_out = lax.optimization_barrier(placed(jnp.zeros((rows, half), BF16), 0, [(c * parts + k, dx_keeps[k]) for k in range(parts)]))
        m_d, m_e, m_got, n_a, n_b, n_got = lax.optimization_barrier((m_d, m_e, m_got, n_a, n_b, n_got, y_keep))[:6]
        dwd = placed(jnp.zeros((ffn, half), BF16), 0, [
            (r * 2 + d, pick(diag, m_d, n_a)),
            (r * 2 + 1 - d, pick(diag, m_e, n_got[0])),
            ((1 - r) * 2 + d, pick(diag, m_got[0], n_b)),
            ((1 - r) * 2 + 1 - d, pick(diag, m_got[1], n_got[1])),
        ])

        dwd = lax.optimization_barrier(dwd)
        hn, hf, bn, bf = [a0 + a1 for a0, a1 in zip(*sums_k)]
        at_c = (jnp.arange(2) == c).astype(F32)[:, None]

        def slots(near, far):
            return (at_c * near + (1.0 - at_c) * far).reshape(-1)

        sums = jnp.concatenate([slots(hn, hf), slots(bn, bf), (at_c * dbu).reshape(-1), (at_c * dbd).reshape(-1)])
        sums = lax.psum(after(sums, y_keep, y_out, dx_out, dwd), ('depth', 'col', 'row'))
        dx_out = placed(dx_out, 0, [((1 - c) * parts + k, dx_gives[k]) for k in range(parts)])

        def sums_at(base, size):
            return lax.dynamic_slice_in_dim(sums, base + c * size, size, 0)

        dgam, dbet = sums_at(0, half), sums_at(width, half)
        dbu, dbd = sums_at(2 * width, ffn), sums_at(2 * width + 2 * ffn, half)
        return y_out, dx_out, dgam, dbet, dwu, dbu, dwd, dbd

    return jax.shard_map(
        local_pass,
        mesh=mesh,
        in_specs=(tok_spec, vec_spec, vec_spec, mat_spec, vec_spec, mat_spec, vec_spec, tok_spec),
        out_specs=(tok_spec, tok_spec, grad_vec, grad_vec, grad_mat, grad_vec, grad_mat, grad_vec),
        check_vma=False,
    )
```

time: 3920 us -> 1510 us (0.39)
  waiting for transfers between devices: 2530 us -> 470 us
  blocking collectives: 795 us -> 45.5 us
  matrix products: 528 us -> 759 us
  other arithmetic: 45.8 us -> 120 us
  local copies, waits for them, and re-layouts: 1.68 us -> 54.7 us
    reduce_scatter x4 -> x0, waiting for transfers between devices: 1780 us -> none  [the longest x1 1450 us: local_pass(): lax.psum_scatter(hidden_part, 'col', scatter_dimension=1, tiled=True)]
    psum x5 -> x1, blocking collectives: 795 us -> 39.7 us  [local_pass(): lax.psum(after(sums, y_keep, y_out, dx_out, dwd), ('depth', 'col', 'row'))]
    all_gather x4 -> x5, waiting for transfers between devices: 749 us -> 4.22 us  [the longest x1 4.21 us: local_pass(): d_mine = lax.all_gather(w_down, 'row', axis=0, tiled=True)]
    ppermute x0 -> x22, waiting for transfers between devices: none -> 466 us  [hop(): return lax.ppermute(value, axis, pairs)]
    dot_general x6 -> x21, matrix products: 528 us -> 759 us  [mm(): return lax.dot_general(a, b, (dims, ((), ())), preferred_element_type=F32)]
  transfers between devices with their start and end apart: 8 -> 27, of which waited for: 5 -> 7; matrix products, arithmetic and copies ran while one was open for 11% -> 62% of each run, Pallas kernels for 0% -> 0%
where the time goes in v1:
time: 1510 us; the launch traced here: 1500 us
  matrix products  759 us (50%)
  waiting for transfers between devices  470 us (31%)
  other arithmetic  120 us (8%)
  local copies, waits for them, and re-layouts  54.7 us (4%)
  blocking collectives  45.5 us (3%)
  starting transfers between devices  39.2 us (3%)
  between operations  16.1 us (1%)
    dot_general x21, matrix products, mm(): return lax.dot_general(a, b, (dims, ((), ())), preferred_element_type=F32)  759 us
    ppermute x22, waiting for transfers between devices, hop(): return lax.ppermute(value, axis, pairs)  466 us
    psum x1, blocking collectives, local_pass(): lax.psum(after(sums, y_keep, y_out, dx_out, dwd), ('depth', 'col', 'row'))  39.7 us
    ppermute x22, starting transfers between devices, hop(): return lax.ppermute(value, axis, pairs)  39 us
    dynamic_update_slice x8, other arithmetic, placed(): lax.dynamic_update_slice_in_dim(out, value, index * value.shape[axis], axis)  38 us
  transfers between devices with their start and end apart: 27, of which 7 were waited for; matrix products, arithmetic and copies ran while one was open for 62% of the time, Pallas kernels for 0%

profile of v1, /device:TPU:0, one launch (start us, length us, event | category | flops | bytes accessed | tf_op | source)
XLA Modules:
  0.0 1504.2 jit_solution(10089905488422219842)
XLA Ops:
  45.0 45.3 %fusion.65 = f32[4096,4096]{1,0:T(8,128)} fusion(bf16[4096,1024]{1,0:T(8,128)(2,1)} %param.15, bf16[8192,1024]{1,0:T(8,128)(2,1)} %all-gather.7.cloned.1.call-done, s32[]{:T(128)S(6)} %select_n.137), kind=kOutput, calls=%fused_computation.88 | convolution fusion | flops 34359738368 | bytes 83886080 | tf_op jit(solution)/shard_map/dot_general | solution.py:25
  90.3 25.2 %fusion.62 = f32[2048,4096]{1,0:T(8,128)} fusion(bf16[8192,1024]{1,0:T(8,128)(2,1)} %all-gather.7.cloned.1.call-done, s32[]{:T(128)S(6)} %select_n.138, bf16[4096,1024]{1,0:T(8,128)(2,1)} %param.15, s32[]{:T(128)S(6)} %select_n.136), kind=kOutput, calls=%fused_computation.85 | convolution fusion | flops 17179869184 | bytes 46137352 | tf_op jit(solution)/shard_map/dot_general | solution.py:25
  115.5 88.6 %collective-permute-done = bf16[4096,1024]{1,0:T(8,128)(2,1)} collective-permute-done((bf16[4096,1024]{1,0:T(8,128)(2,1)}, bf16[4096,1024]{1,0:T(8,128)(2,1)}, u32[]{:S(2)}, u32[]{:S(2)}) %collective-permute-start) | collective-permute-done | bytes 8388640 | tf_op jit(solution)/shard_map/ppermute | solution.py:55
  238.6 99.4 %fusion.3 = (bf16[4096,4096]{1,0:T(8,128)(2,1)}, bf16[4096,4096]{1,0:T(8,128)(2,1)}) fusion(f32[4096]{0:T(1024)S(1)} %convert_element_type.123, bf16[4096,2048]{1,0:T(8,128)(2,1)} %fusion.50, bf16[2048,4096]{1,0:T(8,128)(2,1)} %all-gather.9.cloned.1.call-done), kind=kOutput, calls=%fused_computation.7 | convolution fusion | flops 68920803328 | bytes 100679680 | tf_op jit(solution)/shard_map/dot_general | solution.py:25
  338.0 24.4 %fusion.48 = f32[2048,1024]{1,0:T(8,128)} fusion(bf16[4096,1024]{1,0:T(8,128)(2,1)} %param.15, bf16[4096,4096]{1,0:T(8,128)(2,1)} %get-tuple-element.68, s32[]{:T(128)S(6)} %select_n.142), kind=kOutput, calls=%fused_computation.65 | convolution fusion | flops 17179869184 | bytes 33554436 | tf_op jit(solution)/shard_map/dot_general | solution.py:25
  365.0 25.1 %fusion.46 = f32[2048,1024]{1,0:T(8,128)} fusion(bf16[4096,4096]{1,0:T(8,128)(2,1)} %get-tuple-element.68, s32[]{:T(128)S(6)} %select_n.136, bf16[8192,1024]{1,0:T(8,128)(2,1)} %all-gather.7.cloned.1.call-done, s32[]{:T(128)S(6)} %select_n.137), kind=kOutput, calls=%fused_computation.63 | convolution fusion | flops 17179869184 | bytes 33554440 | tf_op jit(solution)/shard_map/dot_general | solution.py:25
  390.1 24.8 %fusion.67 = f32[2048,1024]{1,0:T(8,128)} fusion(f32[2048,1024]{1,0:T(8,128)} %collective-permute-done.2, bf16[4096,1024]{1,0:T(8,128)(2,1)} %param.15, bf16[4096,4096]{1,0:T(8,128)(2,1)} %get-tuple-element.68, s32[]{:T(128)S(6)} %select_n.143), kind=kOutput, calls=%fused_computation.92 | convolution fusion | flops 17181966336 | bytes 41943044 | tf_op jit(solution)/shard_map/dot_general | solution.py:25
  414.8 131.8 %collective-permute-done.1 = bf16[4096,1024]{1,0:T(8,128)(2,1)} collective-permute-done((bf16[4096,1024]{1,0:T(8,128)(2,1)}, bf16[4096,1024]{1,0:T(8,128)(2,1)}, u32[]{:S(2)}, u32[]{:S(2)}) %collective-permute-start.1) | collective-permute-done | bytes 8388640 | tf_op jit(solution)/shard_map/ppermute | solution.py:55
  546.6 85.9 %convert_reduce_fusion = (f32[4096]{0:T(1024)S(1)}, bf16[4096,4096]{1,0:T(8,128)(2,1)}) fusion(bf16[4096,4096]{1,0:T(8,128)(2,1)} %get-tuple-element.122, f32[4096,4096]{1,0:T(8,128)} %fusion.65, bf16[4096,1024]{1,0:T(8,128)(2,1)} %collective-permute-done.1, bf16[4096,1024]{1,0:T(8,128)(2,1)} %all-gather.11.cloned.1.call-done), kind=kOutput, calls=%fused_computation.16 | convolution fusion | flops 34712055808 | bytes 151011328 | tf_op jit(solution)/shard_map/dot_general | solution.py:25
  632.5 24.0 %fusion.42 = f32[2048,1024]{1,0:T(8,128)} fusion(bf16[4096,1024]{1,0:T(8,128)(2,1)} %collective-permute-done.1, bf16[4096,4096]{1,0:T(8,128)(2,1)} %get-tuple-element.68, s32[]{:T(128)S(6)} %select_n.142), kind=kOutput, calls=%fused_computation.59 | convolution fusion | flops 17179869184 | bytes 33554436 | tf_op jit(solution)/shard_map/dot_general | solution.py:25
  656.6 69.4 %collective-permute-done.8 = bf16[1024,4096]{1,0:T(8,128)(2,1)} collective-permute-done((bf16[1024,4096]{1,0:T(8,128)(2,1)}, bf16[1024,4096]{1,0:T(8,128)(2,1)}, u32[]{:S(2)}, u32[]{:S(2)}) %collective-permute-start.8) | collective-permute-done | bytes 8388640 | tf_op jit(solution)/shard_map/ppermute | solution.py:55
  734.9 26.8 %fusion.82 = f32[512,4096]{1,0:T(8,128)} fusion(bf16[4096,4096]{1,0:T(8,128)(2,1)} %get-tuple-element.67, bf16[4096,2048]{1,0:T(8,128)(2,1)} %fusion.50, s32[]{:T(128)S(6)} %select_n.148), kind=kOutput, calls=%fused_computation.119 | convolution fusion | flops 17179869184 | bytes 46137348 | tf_op jit(solution)/shard_map/dot_general | solution.py:25
  791.4 27.0 %fusion.80 = f32[512,4096]{1,0:T(8,128)} fusion(bf16[4096,4096]{1,0:T(8,128)(2,1)} %get-tuple-element.67, bf16[4096,2048]{1,0:T(8,128)(2,1)} %fusion.50, s32[]{:T(128)S(6)} %select_n.149), kind=kOutput, calls=%fused_computation.117 | convolution fusion | flops 17179869184 | bytes 46137348 | tf_op jit(solution)/shard_map/dot_general | solution.py:25
  821.5 38.8 %collective-permute-done.13 = f32[1024,1024]{1,0:T(8,128)} collective-permute-done((f32[1024,1024]{1,0:T(8,128)}, f32[1024,1024]{1,0:T(8,128)}, u32[]{:S(2)}, u32[]{:S(2)}) %collective-permute-start.13) | collective-permute-done | bytes 4194336 | tf_op jit(solution)/shard_map/ppermute | solution.py:55
  869.3 125.3 %collective-permute-done.14 = bf16[1024,1024]{1,0:T(8,128)(2,1)} collective-permute-done((bf16[1024,1024]{1,0:T(8,128)(2,1)S(1)}, bf16[1024,1024]{1,0:T(8,128)(2,1)}, u32[]{:S(2)}, u32[]{:S(2)}) %collective-permute-start.14) | collective-permute-done | bytes 2097184 | tf_op jit(solution)/shard_map/ppermute | solution.py:55
  1011.3 28.1 %convolution_add_fusion.1 = f32[512,4096]{1,0:T(8,128)} fusion(f32[512,4096]{1,0:T(8,128)} %collective-permute-done.6, bf16[4096,4096]{1,0:T(8,128)(2,1)} %get-tuple-element.67, bf16[4096,2048]{1,0:T(8,128)(2,1)} %fusion.50, s32[]{:T(128)S(6)} %select_n.150), kind=kOutput, calls=%fused_computation.91 | convolution fusion | flops 17181966336 | bytes 54525956 | tf_op jit(solution)/shard_map/dot_general | solution.py:25
  1061.0 28.3 %convolution_add_fusion = f32[512,4096]{1,0:T(8,128)} fusion(f32[512,4096]{1,0:T(8,128)} %collective-permute-done.7, bf16[4096,4096]{1,0:T(8,128)(2,1)} %get-tuple-element.67, bf16[4096,2048]{1,0:T(8,128)(2,1)} %fusion.50, s32[]{:T(128)S(6)} %select_n.151), kind=kOutput, calls=%fused_computation.90 | convolution fusion | flops 17181966336 | bytes 54525956 | tf_op jit(solution)/shard_map/dot_general | solution.py:25
  1089.3 45.0 %fusion.38 = f32[2048,2048]{1,0:T(8,128)} fusion(bf16[2048,4096]{1,0:T(8,128)(2,1)} %all-gather.9.cloned.1.call-done, bf16[4096,4096]{1,0:T(8,128)(2,1)} %get-tuple-element.67, s32[]{:T(128)S(6)} %select_n.136), kind=kOutput, calls=%fused_computation.55 | convolution fusion | flops 34359738368 | bytes 50331652 | tf_op jit(solution)/shard_map/dot_general | solution.py:25
  1158.3 52.6 %fusion.15 = (bf16[2048,4096]{1,0:T(8,128)(2,1)}, bf16[2048,4096]{1,0:T(8,128)(2,1)}) fusion(f32[4096]{0:T(1024)S(1)} %bitcast.109, bf16[2048,4096]{1,0:T(8,128)(2,1)} %all-gather.13.cloned.1.call-done, bf16[4096,2048]{1,0:T(8,128)(2,1)} %fusion.50, s32[]{:T(128)S(6)} %select_n.136), kind=kOutput, calls=%fused_computation.25 | convolution fusion | flops 34460401664 | bytes 58736644 | tf_op jit(solution)/shard_map/dot_general | solution.py:25
  1210.9 29.3 %add_convert_fusion.4 = bf16[2048,1024]{1,0:T(8,128)(2,1)} fusion(f32[2048,1024]{1,0:T(8,128)} %fusion.36, f32[1024]{0:T(1024)S(1)} %bitcast.110, bf16[4096,1024]{1,0:T(8,128)(2,1)} %collective-permute-done, s32[]{:T(128)S(6)} %select_n.136, bf16[8192,1024]{1,0:T(8,128)(2,1)} %all-gather.15.cloned.1.call-done, s32[]{:T(128)S(6)} %select_n.138, ...), kind=kOutput, calls=%fused_computation.78 | convolution fusion | flops 17274241024 | bytes 41947144 | tf_op jit(solution)/shard_map/dot_general | solution.py:25
  1245.8 45.7 %fusion.19 = bf16[2048,4096]{1,0:T(8,128)(2,1)} fusion(bf16[2048,4096]{1,0:T(8,128)(2,1)} %get-tuple-element.126, f32[2048,4096]{1,0:T(8,128)} %fusion.62, bf16[8192,1024]{1,0:T(8,128)(2,1)} %all-gather.15.cloned.1.call-done, s32[]{:T(128)S(6)} %select_n.138, bf16[4096,1024]{1,0:T(8,128)(2,1)} %collective-permute-done.1, s32[]{:T(128)S(6)} %select_n.136), kind=kOutput, calls=%fused_computation.29 | convolution fusion | flops 17339252736 | bytes 79691784 | tf_op jit(solution)/shard_map/dot_general | solution.py:25
  1335.2 25.6 %slice_add_fusion.1 = f32[1024,2048]{1,0:T(8,128)} fusion(f32[2048,2048]{1,0:T(8,128)} %fusion.38, bf16[2048,4096]{1,0:T(8,128)(2,1)} %all-gather.13.cloned.1.call-done, bf16[2048,4096]{1,0:T(8,128)(2,1)} %fusion.19), kind=kOutput, calls=%fused_computation.71 | convolution fusion | flops 17181966336 | bytes 41943040 | tf_op jit(solution)/shard_map/dot_general | solution.py:25
  1371.8 24.7 %add_convert_fusion.3 = bf16[2048,1024]{1,0:T(8,128)(2,1)} fusion(f32[2048,1024]{1,0:T(8,128)} %fusion.46, f32[1024]{0:T(1024)S(1)} %copy-done.26, bf16[4096,1024]{1,0:T(8,128)(2,1)S(1)} %bitcast.76, s32[]{:T(128)S(6)} %select_n.136, bf16[2048,4096]{1,0:T(8,128)(2,1)} %get-tuple-element.77, bf16[8192,1024]{1,0:T(8,128)(2,1)} %all-gather.7.cloned.1.call-done, ...), kind=kOutput, calls=%fused_computation.73 | convolution fusion | flops 17190354944 | bytes 41947144 | tf_op jit(solution)/shard_map/dot_general | solution.py:25
  1445.0 39.7 %psum.7 = f32[14336]{0:T(1024)S(1)} all-reduce(f32[14336]{0:T(1024)S(1)} %pad_maximum_fusion.2), channel_id=1, replica_groups=mesh['dp'=1,'depth'=2,'col'=2,'row'=2] {'depth','col','row'}, use_global_device_ids=true, to_apply=%region_22.23 | all-reduce | flops 14336 | bytes 114688 | tf_op jit(solution)/shard_map/psum | solution.py:215
  (201 shorter events, 307.0 us)
Async XLA Ops:
  16.0 222.6 %all-gather.9.cloned.1.call-start = ((), (), s32[]{:S(2)}) async-start(), calls=%async_computation.1 | async-start | bytes 25165824 | tf_op jit(solution)/shard_map/all_gather | solution.py:92
  20.4 183.7 %collective-permute-start = (bf16[4096,1024]{1,0:T(8,128)(2,1)}, bf16[4096,1024]{1,0:T(8,128)(2,1)}, u32[]{:S(2)}, u32[]{:S(2)}) collective-permute-start(bf16[4096,1024]{1,0:T(8,128)(2,1)} %param.8), channel_id=1, source_target_pairs={{0,2},{2,0},{1,3},{3,1},{4,6},{6,4},{5,7},{7,5}} | collective-permute-start | bytes 25165832 | tf_op jit(solution)/shard_map/ppermute | solution.py:55
  22.7 523.9 %all-gather.11.cloned.1.call-start = ((), (), s32[]{:S(2)}) async-start(), calls=%async_computation.2 | async-start | bytes 10485760 | tf_op jit(solution)/shard_map/all_gather | solution.py:93
  40.1 322.8 %collective-permute-start.4 = (bf16[1024,1024]{1,0:T(8,128)(2,1)}, bf16[1024,1024]{1,0:T(8,128)(2,1)}, u32[]{:S(2)}, u32[]{:S(2)}) collective-permute-start(bf16[1024,1024]{1,0:T(8,128)(2,1)} %dynamic-slice_select_fusion), channel_id=1, source_target_pairs={{0,2},{2,0},{1,3},{3,1},{4,6},{6,4},{5,7},{7,5}} | collective-permute-start | bytes 6291464 | tf_op jit(solution)/shard_map/ppermute | solution.py:55
  362.9 795.4 %all-gather.13.cloned.1.call-start = ((), (), s32[]{:S(2)}) async-start(), calls=%async_computation.3 | async-start | bytes 25165824 | tf_op jit(solution)/shard_map/all_gather | solution.py:95
  362.9 183.7 %collective-permute-start.1 = (bf16[4096,1024]{1,0:T(8,128)(2,1)}, bf16[4096,1024]{1,0:T(8,128)(2,1)}, u32[]{:S(2)}, u32[]{:S(2)}) collective-permute-start(bf16[4096,1024]{1,0:T(8,128)(2,1)} %param.15), channel_id=1, source_target_pairs={{0,2},{2,0},{1,3},{3,1},{4,6},{6,4},{5,7},{7,5}} | collective-permute-start | bytes 25165832 | tf_op jit(solution)/shard_map/ppermute | solution.py:55
  364.8 361.2 %collective-permute-start.8 = (bf16[1024,4096]{1,0:T(8,128)(2,1)}, bf16[1024,4096]{1,0:T(8,128)(2,1)}, u32[]{:S(2)}, u32[]{:S(2)}) collective-permute-start(bf16[1024,4096]{1,0:T(8,128)(2,1)} %param.11), channel_id=1, source_target_pairs={{0,2},{2,0},{1,3},{3,1},{4,6},{6,4},{5,7},{7,5}} | collective-permute-start | bytes 25165832 | tf_op jit(solution)/shard_map/ppermute | solution.py:55
  656.6 111.5 %collective-permute-start.5 = (f32[2048,1024]{1,0:T(8,128)}, f32[2048,1024]{1,0:T(8,128)}, u32[]{:S(2)}, u32[]{:S(2)}) collective-permute-start(f32[2048,1024]{1,0:T(8,128)} %fusion.42), channel_id=1, source_target_pairs={{0,1},{1,0},{2,3},{3,2},{4,5},{5,4},{6,7},{7,6}} | collective-permute-start | bytes 25165832 | tf_op jit(solution)/shard_map/ppermute | solution.py:55
  726.0 484.9 %all-gather.15.cloned.1.call-start = ((), (), s32[]{:S(2)}) async-start(), calls=%async_computation.4 | async-start | bytes 25165824 | tf_op jit(solution)/shard_map/all_gather | solution.py:94
  726.1 141.3 %collective-permute-start.9 = (bf16[4096,1024]{1,0:T(8,128)(2,1)}, bf16[4096,1024]{1,0:T(8,128)(2,1)}, u32[]{:S(2)}, u32[]{:S(2)}) collective-permute-start(bf16[4096,1024]{1,0:T(8,128)(2,1)} %param.13), channel_id=1, source_target_pairs={{0,2},{3,1},{4,6},{7,5}} | collective-permute-start | bytes 25165832 | tf_op jit(solution)/shard_map/ppermute | solution.py:55
  761.7 249.7 %collective-permute-start.6 = (f32[512,4096]{1,0:T(8,128)}, f32[512,4096]{1,0:T(8,128)}, u32[]{:S(2)}, u32[]{:S(2)}) collective-permute-start(f32[512,4096]{1,0:T(8,128)} %fusion.82), channel_id=1, source_target_pairs={{0,1},{1,0},{2,3},{3,2},{4,5},{5,4},{6,7},{7,6}} | collective-permute-start | bytes 25165832 | tf_op jit(solution)/shard_map/ppermute | solution.py:55
  766.5 93.8 %collective-permute-start.13 = (f32[1024,1024]{1,0:T(8,128)}, f32[1024,1024]{1,0:T(8,128)}, u32[]{:S(2)}, u32[]{:S(2)}) collective-permute-start(f32[1024,1024]{1,0:T(8,128)} %constant_dynamic-slice_fusion.4), channel_id=1, source_target_pairs={{0,4},{4,0},{1,5},{5,1},{2,6},{6,2},{3,7},{7,3}} | collective-permute-start | bytes 12582920 | tf_op jit(solution)/shard_map/ppermute | solution.py:55
  818.4 242.5 %collective-permute-start.7 = (f32[512,4096]{1,0:T(8,128)}, f32[512,4096]{1,0:T(8,128)}, u32[]{:S(2)}, u32[]{:S(2)}) collective-permute-start(f32[512,4096]{1,0:T(8,128)} %fusion.80), channel_id=1, source_target_pairs={{0,1},{1,0},{2,3},{3,2},{4,5},{5,4},{6,7},{7,6}} | collective-permute-start | bytes 25165832 | tf_op jit(solution)/shard_map/ppermute | solution.py:55
  820.9 179.3 %collective-permute-start.16 = (f32[1024,1024]{1,0:T(8,128)}, f32[1024,1024]{1,0:T(8,128)}, u32[]{:S(2)}, u32[]{:S(2)}) collective-permute-start(f32[1024,1024]{1,0:T(8,128)} %constant_dynamic-slice_fusion.3), channel_id=1, source_target_pairs={{0,4},{4,0},{1,5},{5,1},{2,6},{6,2},{3,7},{7,3}} | collective-permute-start | bytes 12582920 | tf_op jit(solution)/shard_map/ppermute | solution.py:55
  864.5 130.2 %collective-permute-start.14 = (bf16[1024,1024]{1,0:T(8,128)(2,1)S(1)}, bf16[1024,1024]{1,0:T(8,128)(2,1)}, u32[]{:S(2)}, u32[]{:S(2)}) collective-permute-start(bf16[1024,1024]{1,0:T(8,128)(2,1)S(1)} %add_convert_fusion.6), channel_id=1, source_target_pairs={{0,4},{4,0},{1,5},{5,1},{2,6},{6,2},{3,7},{7,3}} | collective-permute-start | bytes 6291464 | tf_op jit(solution)/shard_map/ppermute | solution.py:55
  998.6 420.1 %collective-permute-start.15 = (bf16[2,1024,1024]{2,1,0:T(8,128)(2,1)}, bf16[2,1024,1024]{2,1,0:T(8,128)(2,1)}, u32[]{:S(2)}, u32[]{:S(2)}) collective-permute-start(bf16[2,1024,1024]{2,1,0:T(8,128)(2,1)} %pad_maximum_fusion), channel_id=1, source_target_pairs={{1,0},{2,3},{5,4},{6,7}} | collective-permute-start | bytes 12582920 | tf_op jit(solution)/shard_map/ppermute | solution.py:55
  1005.8 47.6 %collective-permute-start.17 = (bf16[1024,1024]{1,0:T(8,128)(2,1)}, bf16[1024,1024]{1,0:T(8,128)(2,1)}, u32[]{:S(2)}, u32[]{:S(2)}) collective-permute-start(bf16[1024,1024]{1,0:T(8,128)(2,1)} %add_convert_fusion.5), channel_id=1, source_target_pairs={{0,2},{3,1},{4,6},{7,5}} | collective-permute-start | bytes 6291464 | tf_op jit(solution)/shard_map/ppermute | solution.py:55
  1010.5 42.8 %collective-permute-start.18 = (bf16[1024,1024]{1,0:T(8,128)(2,1)}, bf16[1024,1024]{1,0:T(8,128)(2,1)S(1)}, u32[]{:S(2)}, u32[]{:S(2)}) collective-permute-start(bf16[1024,1024]{1,0:T(8,128)(2,1)} %add_convert_fusion.5), channel_id=1, source_target_pairs={{1,2},{2,1},{5,6},{6,5}} | collective-permute-start | bytes 6291464 | tf_op jit(solution)/shard_map/ppermute | solution.py:55
  1039.5 286.2 %collective-permute-start.20 = (f32[512,4096]{1,0:T(8,128)}, f32[512,4096]{1,0:T(8,128)}, u32[]{:S(2)}, u32[]{:S(2)}) collective-permute-start(f32[512,4096]{1,0:T(8,128)} %convolution_add_fusion.1), channel_id=1, source_target_pairs={{0,4},{4,0},{1,5},{5,1},{2,6},{6,2},{3,7},{7,3}} | collective-permute-start | bytes 25165832 | tf_op jit(solution)/shard_map/ppermute | solution.py:55
  1058.1 362.7 %collective-permute-start.19 = (bf16[2,1024,1024]{2,1,0:T(8,128)(2,1)}, bf16[2,1024,1024]{2,1,0:T(8,128)(2,1)}, u32[]{:S(2)}, u32[]{:S(2)}) collective-permute-start(bf16[2,1024,1024]{2,1,0:T(8,128)(2,1)} %pad_maximum_fusion.1), channel_id=1, source_target_pairs={{1,5},{5,1},{2,6},{6,2}} | collective-permute-start | bytes 12582920 | tf_op jit(solution)/shard_map/ppermute | solution.py:55
  1240.3 200.1 %collective-permute-start.10 = (bf16[2048,1024]{1,0:T(8,128)(2,1)}, bf16[2048,1024]{1,0:T(8,128)(2,1)}, u32[]{:S(2)}, u32[]{:S(2)}) collective-permute-start(bf16[2048,1024]{1,0:T(8,128)(2,1)} %add_convert_fusion.4), channel_id=1, source_target_pairs={{0,2},{2,0},{1,3},{3,1},{4,6},{6,4},{5,7},{7,5}} | collective-permute-start | bytes 12582920 | tf_op jit(solution)/shard_map/ppermute | solution.py:55
  1325.7 160.3 %collective-permute-start.11 = (bf16[1024,1024]{1,0:T(8,128)(2,1)S(1)}, bf16[1024,1024]{1,0:T(8,128)(2,1)}, u32[]{:S(2)}, u32[]{:S(2)}) collective-permute-start(bf16[1024,1024]{1,0:T(8,128)(2,1)S(1)} %add_convert_fusion.10), channel_id=1, source_target_pairs={{0,2},{2,0},{1,3},{3,1},{4,6},{6,4},{5,7},{7,5}} | collective-permute-start | bytes 6291464 | tf_op jit(solution)/shard_map/ppermute | solution.py:55
  1334.8 154.2 %collective-permute-start.21 = (bf16[512,4096]{1,0:T(8,128)(2,1)}, bf16[512,4096]{1,0:T(8,128)(2,1)}, u32[]{:S(2)}, u32[]{:S(2)}) collective-permute-start(bf16[512,4096]{1,0:T(8,128)(2,1)} %add_convert_fusion.2), channel_id=1, source_target_pairs={{0,4},{4,0},{1,5},{5,1},{2,6},{6,2},{3,7},{7,3}} | collective-permute-start | bytes 12582920 | tf_op jit(solution)/shard_map/ppermute | solution.py:55
  1418.7 75.0 %collective-permute-start.12 = (bf16[1024,1024]{1,0:T(8,128)(2,1)}, bf16[1024,1024]{1,0:T(8,128)(2,1)}, u32[]{:S(2)}, u32[]{:S(2)}) collective-permute-start(bf16[1024,1024]{1,0:T(8,128)(2,1)} %add_convert_fusion.9), channel_id=1, source_target_pairs={{0,2},{2,0},{1,3},{3,1},{4,6},{6,4},{5,7},{7,5}} | collective-permute-start | bytes 6291464 | tf_op jit(solution)/shard_map/ppermute | solution.py:55
  (41 other events, 1194.0 us)
Sparse Core Ops, SparseCore 0:
  16.1 28.8 all-gather.6
  46.5 28.4 all-gather.8
  726.1 28.5 all-gather.12
  867.5 26.3 all-gather.14
Sparse Core Ops, SparseCore 1:
  363.0 56.7 all-gather.10

commit v2 on v1

--- a/solution.py
+++ b/solution.py
@@ -85,6 +85,9 @@
         u_got = hop('col', w_up)
         d_rest = hop(('col', 'row'), w_down, [(0, 2), (3, 1)])
 
+        shapes = ((rows, half), (rows, half), (ffn, half), (half, ffn), (rows, width))
+        y_base, dx_base, dwd_base, dwu_base, xn_base = [jnp.full(shape, k, BF16) for k, shape in enumerate(shapes)]
+
         def own_rows(v):
             return rows_of(v, c, own)
 
@@ -114,7 +117,7 @@
         def normed(v, g, b):
             return (((v.astype(F32) - mu) * inv) * g + b).astype(BF16)
 
-        xn = placed(jnp.zeros((rows, width), BF16), 1, [(c, normed(x, gamma, beta)), (1 - c, normed(x_peer, gam_peer, bet_peer))])
+        xn = placed(xn_base, 1, [(c, normed(x, gamma, beta)), (1 - c, normed(x_peer, gam_peer, bet_peer))])
         xn = after(xn, da_o)
 
         u_c = (mm(xn, w_up_c, NN) + b_up.astype(F32)).astype(BF16)
@@ -132,7 +135,7 @@
         dbu = jnp.sum(du_c.astype(F32), axis=0)
         du_c, dbu = lax.optimization_barrier((du_c, dbu))
         m_e = hop('depth', m_d)
-        m_got = hop(('col', 'row'), jnp.stack([m_d, m_e]), [(1, 0), (2, 3)])
+        m_got = [hop(('col', 'row'), v, [(1, 0), (2, 3)]) for v in (m_d, m_e)]
 
         e = width // 4
         give = lax.optimization_barrier(mm(cols_of(after(a_c, du_c), 1 - r, f2), dy_peer, TN))
@@ -148,11 +151,10 @@
         q4 = lax.optimization_barrier(mm(cols_of(after(xn, q3), r * 2 + d, e), du_c, TN) + g2)
         dwu_d = lax.optimization_barrier((q4 + got).astype(BF16))
         dwu_e = hop('depth', dwu_d)
-        dwu = placed(lax.optimization_barrier(placed(jnp.zeros((half, ffn), BF16), 0, [(d, dwu_d)])), 0, [(1 - d, dwu_e)])
 
         n_a = hop(('col', 'row'), n_d, [(0, 2), (3, 1)])
         n_b = hop(('col', 'row'), n_d, [(1, 2), (2, 1)])
-        n_got = hop(('depth', 'col', 'row'), jnp.stack([n_a, n_b]), [(1, 5), (5, 1), (2, 6), (6, 2)])
+        n_got = [hop(('depth', 'col', 'row'), v, [(1, 5), (5, 1), (2, 6), (6, 2)]) for v in (n_a, n_b)]
         dxn_c = lax.optimization_barrier(mm(own_rows(after(du_c, q4)), w_up_c, NT))
         yp_c = lax.optimization_barrier(mm(own_rows(after(a_c, dxn_c)), dp_c, NN))
 
@@ -186,6 +188,10 @@
             mp = (jnp.sum(g_near * h_near, 1, keepdims=True) + jnp.sum(g_far * h_far, 1, keepdims=True)) * inv_width
             sums_k.append([jnp.sum(near * h_near, 0), jnp.sum(far * h_far, 0), jnp.sum(near, 0), jnp.sum(far, 0)])
             mg, mp = lax.optimization_barrier((mg, mp))
+            if k == parts - 1:
+                hn, hf, bn, bf = [sum(terms[1:], terms[0]) for terms in zip(*sums_k)]
+                near_sums = jnp.concatenate([hn, bn])
+                far_got = hop('col', jnp.concatenate([hf, bf]))
             dx_far = (dyr_own[cut].astype(F32) + ik * (g_far - mg - h_far * mp)).astype(BF16)
             prev = dx_far = lax.optimization_barrier(dx_far)
             dx_gives.append(hop('col', dx_far))
@@ -194,10 +200,11 @@
         a_l = after(a_o, prev)
         y_keep = ((x_own.astype(F32) + (ym_c + mm(a_l, dm_o, NN))) + bd_mine).astype(BF16)
         y_keep = lax.optimization_barrier(y_keep)
-        y_out = lax.optimization_barrier(placed(jnp.zeros((rows, half), BF16), 0, [(c, y_keep), (1 - c, y_got)]))
-        dx_out = lax.optimization_barrier(placed(jnp.zeros((rows, half), BF16), 0, [(c * parts + k, dx_keeps[k]) for k in range(parts)]))
-        m_d, m_e, m_got, n_a, n_b, n_got = lax.optimization_barrier((m_d, m_e, m_got, n_a, n_b, n_got, y_keep))[:6]
-        dwd = placed(jnp.zeros((ffn, half), BF16), 0, [
+        dwu = lax.optimization_barrier(placed(dwu_base, 0, [(d, after(dwu_d, y_keep))]))
+        y_out = lax.optimization_barrier(placed(y_base, 0, [(c, y_keep), (1 - c, y_got)]))
+        dx_out = lax.optimization_barrier(placed(dx_base, 0, [(c * parts + k, after(dx_keeps[k], y_keep)) for k in range(parts)]))
+        m_d, m_e, m_got, n_a, n_b, n_got = lax.optimization_barrier((m_d, m_e, tuple(m_got), n_a, n_b, tuple(n_got), y_keep))[:6]
+        dwd = placed(dwd_base, 0, [
             (r * 2 + d, pick(diag, m_d, n_a)),
             (r * 2 + 1 - d, pick(diag, m_e, n_got[0])),
             ((1 - r) * 2 + d, pick(diag, m_got[0], n_b)),
@@ -205,21 +212,12 @@
         ])
 
         dwd = lax.optimization_barrier(dwd)
-        hn, hf, bn, bf = [a0 + a1 for a0, a1 in zip(*sums_k)]
-        at_c = (jnp.arange(2) == c).astype(F32)[:, None]
-
-        def slots(near, far):
-            return (at_c * near + (1.0 - at_c) * far).reshape(-1)
-
-        sums = jnp.concatenate([slots(hn, hf), slots(bn, bf), (at_c * dbu).reshape(-1), (at_c * dbd).reshape(-1)])
-        sums = lax.psum(after(sums, y_keep, y_out, dx_out, dwd), ('depth', 'col', 'row'))
+        sums = jnp.concatenate([near_sums + far_got, dbu, dbd])
+        sums = lax.psum(after(sums, y_keep, y_out, dx_out, dwd, dwu), ('depth', 'row'))
+        dwu = placed(dwu, 0, [(1 - d, dwu_e)])
         dx_out = placed(dx_out, 0, [((1 - c) * parts + k, dx_gives[k]) for k in range(parts)])
 
-        def sums_at(base, size):
-            return lax.dynamic_slice_in_dim(sums, base + c * size, size, 0)
-
-        dgam, dbet = sums_at(0, half), sums_at(width, half)
-        dbu, dbd = sums_at(2 * width, ffn), sums_at(2 * width + 2 * ffn, half)
+        dgam, dbet, dbu, dbd = jnp.split(sums, (half, width, width + ffn))
         return y_out, dx_out, dgam, dbet, dwu, dbu, dwd, dbd
 
     return jax.shard_map(

time: 1510 us -> 1600 us (1.060)
  waiting for transfers between devices: 470 us -> 592 us
  blocking collectives: 45.5 us -> 18.1 us
    ppermute x22 -> x25, waiting for transfers between devices: 466 us -> 588 us  [hop(): return lax.ppermute(value, axis, pairs)]
    psum x1, blocking collectives: 39.7 us -> 12.3 us  [local_pass(): lax.psum(after(sums, y_keep, y_out, dx_out, dwd, dwu), ('depth', 'row'))]
    dynamic_update_slice x8 -> x6, other arithmetic: 38 us -> 25 us  [placed(): lax.dynamic_update_slice_in_dim(out, value, index * value.shape[axis], axis)]
    ppermute x22 -> x25, starting transfers between devices: 39 us -> 42.4 us  [hop(): return lax.ppermute(value, axis, pairs)]
  transfers between devices with their start and end apart: 27 -> 30, of which waited for: 7 -> 8; matrix products, arithmetic and copies ran while one was open for 62% -> 58% of each run, Pallas kernels for 0% -> 0%
where the time goes in v2:
time: 1600 us; the launch traced here: 1590 us
  matrix products  760 us (48%)
  waiting for transfers between devices  592 us (37%)
  other arithmetic  105 us (7%)
  local copies, waits for them, and re-layouts  61.5 us (4%)
  starting transfers between devices  42.6 us (3%)
  blocking collectives  18.1 us (1%)
  between operations  16 us (1%)
    dot_general x21, matrix products, mm(): return lax.dot_general(a, b, (dims, ((), ())), preferred_element_type=F32)  760 us
    ppermute x25, waiting for transfers between devices, hop(): return lax.ppermute(value, axis, pairs)  588 us
    ppermute x25, starting transfers between devices, hop(): return lax.ppermute(value, axis, pairs)  42.4 us
  transfers between devices with their start and end apart: 30, of which 8 were waited for; matrix products, arithmetic and copies ran while one was open for 58% of the time, Pallas kernels for 0%

profile of v2, /device:TPU:0, one launch (start us, length us, event | category | flops | bytes accessed | tf_op | source)
XLA Modules:
  0.0 1594.7 jit_solution(7485986817384543968)
XLA Ops:
  45.0 45.3 %fusion.65 = f32[4096,4096]{1,0:T(8,128)} fusion(bf16[4096,1024]{1,0:T(8,128)(2,1)} %param.15, bf16[8192,1024]{1,0:T(8,128)(2,1)} %all-gather.7.cloned.1.call-done, s32[]{:T(128)S(6)} %select_n.120), kind=kOutput, calls=%fused_computation.88 | convolution fusion | flops 34359738368 | bytes 83886080 | tf_op jit(solution)/shard_map/dot_general | solution.py:25
  90.3 25.2 %fusion.62 = f32[2048,4096]{1,0:T(8,128)} fusion(bf16[8192,1024]{1,0:T(8,128)(2,1)} %all-gather.7.cloned.1.call-done, s32[]{:T(128)S(6)} %select_n.121, bf16[4096,1024]{1,0:T(8,128)(2,1)} %param.15, s32[]{:T(128)S(6)} %select_n.119), kind=kOutput, calls=%fused_computation.85 | convolution fusion | flops 17179869184 | bytes 46137352 | tf_op jit(solution)/shard_map/dot_general | solution.py:25
  115.5 88.6 %collective-permute-done = bf16[4096,1024]{1,0:T(8,128)(2,1)} collective-permute-done((bf16[4096,1024]{1,0:T(8,128)(2,1)}, bf16[4096,1024]{1,0:T(8,128)(2,1)}, u32[]{:S(2)}, u32[]{:S(2)}) %collective-permute-start) | collective-permute-done | bytes 8388640 | tf_op jit(solution)/shard_map/ppermute | solution.py:55
  238.6 99.4 %fusion.3 = (bf16[4096,4096]{1,0:T(8,128)(2,1)}, bf16[4096,4096]{1,0:T(8,128)(2,1)}) fusion(f32[4096]{0:T(1024)S(1)} %convert_element_type.113, bf16[4096,2048]{1,0:T(8,128)(2,1)} %fusion.50, bf16[2048,4096]{1,0:T(8,128)(2,1)} %all-gather.9.cloned.1.call-done), kind=kOutput, calls=%fused_computation.7 | convolution fusion | flops 68920803328 | bytes 100679680 | tf_op jit(solution)/shard_map/dot_general | solution.py:25
  338.0 24.4 %fusion.48 = f32[2048,1024]{1,0:T(8,128)} fusion(bf16[4096,1024]{1,0:T(8,128)(2,1)} %param.15, bf16[4096,4096]{1,0:T(8,128)(2,1)} %get-tuple-element.73, s32[]{:T(128)S(6)} %select_n.125), kind=kOutput, calls=%fused_computation.65 | convolution fusion | flops 17179869184 | bytes 33554436 | tf_op jit(solution)/shard_map/dot_general | solution.py:25
  364.9 25.1 %fusion.46 = f32[2048,1024]{1,0:T(8,128)} fusion(bf16[4096,4096]{1,0:T(8,128)(2,1)} %get-tuple-element.73, s32[]{:T(128)S(6)} %select_n.119, bf16[8192,1024]{1,0:T(8,128)(2,1)} %all-gather.7.cloned.1.call-done, s32[]{:T(128)S(6)} %select_n.120), kind=kOutput, calls=%fused_computation.63 | convolution fusion | flops 17179869184 | bytes 33554440 | tf_op jit(solution)/shard_map/dot_general | solution.py:25
  390.0 24.8 %fusion.67 = f32[2048,1024]{1,0:T(8,128)} fusion(f32[2048,1024]{1,0:T(8,128)} %collective-permute-done.2, bf16[4096,1024]{1,0:T(8,128)(2,1)} %param.15, bf16[4096,4096]{1,0:T(8,128)(2,1)} %get-tuple-element.73, s32[]{:T(128)S(6)} %select_n.126), kind=kOutput, calls=%fused_computation.92 | convolution fusion | flops 17181966336 | bytes 41943044 | tf_op jit(solution)/shard_map/dot_general | solution.py:25
  414.8 131.7 %collective-permute-done.1 = bf16[4096,1024]{1,0:T(8,128)(2,1)} collective-permute-done((bf16[4096,1024]{1,0:T(8,128)(2,1)}, bf16[4096,1024]{1,0:T(8,128)(2,1)}, u32[]{:S(2)}, u32[]{:S(2)}) %collective-permute-start.1) | collective-permute-done | bytes 8388640 | tf_op jit(solution)/shard_map/ppermute | solution.py:55
  546.6 86.5 %convert_reduce_fusion = (f32[4096]{0:T(1024)}, bf16[4096,4096]{1,0:T(8,128)(2,1)}) fusion(bf16[4096,4096]{1,0:T(8,128)(2,1)} %get-tuple-element.131, f32[4096,4096]{1,0:T(8,128)} %fusion.65, bf16[4096,1024]{1,0:T(8,128)(2,1)} %collective-permute-done.1, bf16[4096,1024]{1,0:T(8,128)(2,1)} %all-gather.11.cloned.1.call-done), kind=kOutput, calls=%fused_computation.16 | convolution fusion | flops 34712055808 | bytes 151011328 | tf_op jit(solution)/shard_map/dot_general | solution.py:25
  657.1 68.8 %collective-permute-done.8 = bf16[1024,4096]{1,0:T(8,128)(2,1)} collective-permute-done((bf16[1024,4096]{1,0:T(8,128)(2,1)}, bf16[1024,4096]{1,0:T(8,128)(2,1)}, u32[]{:S(2)}, u32[]{:S(2)}) %collective-permute-start.8) | collective-permute-done | bytes 8388640 | tf_op jit(solution)/shard_map/ppermute | solution.py:55
  734.9 26.9 %fusion.82 = f32[512,4096]{1,0:T(8,128)} fusion(bf16[4096,4096]{1,0:T(8,128)(2,1)} %get-tuple-element.72, bf16[4096,2048]{1,0:T(8,128)(2,1)} %fusion.50, s32[]{:T(128)S(6)} %select_n.131), kind=kOutput, calls=%fused_computation.117 | convolution fusion | flops 17179869184 | bytes 46137348 | tf_op jit(solution)/shard_map/dot_general | solution.py:25
  791.4 27.0 %fusion.80 = f32[512,4096]{1,0:T(8,128)} fusion(bf16[4096,4096]{1,0:T(8,128)(2,1)} %get-tuple-element.72, bf16[4096,2048]{1,0:T(8,128)(2,1)} %fusion.50, s32[]{:T(128)S(6)} %select_n.132), kind=kOutput, calls=%fused_computation.115 | convolution fusion | flops 17179869184 | bytes 46137348 | tf_op jit(solution)/shard_map/dot_general | solution.py:25
  821.4 38.9 %collective-permute-done.14 = f32[1024,1024]{1,0:T(8,128)} collective-permute-done((f32[1024,1024]{1,0:T(8,128)}, f32[1024,1024]{1,0:T(8,128)}, u32[]{:S(2)}, u32[]{:S(2)}) %collective-permute-start.14) | collective-permute-done | bytes 4194336 | tf_op jit(solution)/shard_map/ppermute | solution.py:55
  870.7 124.0 %collective-permute-done.15 = bf16[1024,1024]{1,0:T(8,128)(2,1)} collective-permute-done((bf16[1024,1024]{1,0:T(8,128)(2,1)}, bf16[1024,1024]{1,0:T(8,128)(2,1)}, u32[]{:S(2)}, u32[]{:S(2)}) %collective-permute-start.15) | collective-permute-done | bytes 2097184 | tf_op jit(solution)/shard_map/ppermute | solution.py:55
  1006.3 28.3 %convolution_add_fusion.1 = f32[512,4096]{1,0:T(8,128)} fusion(f32[512,4096]{1,0:T(8,128)} %collective-permute-done.6, bf16[4096,4096]{1,0:T(8,128)(2,1)} %get-tuple-element.72, bf16[4096,2048]{1,0:T(8,128)(2,1)} %fusion.50, s32[]{:T(128)S(6)} %select_n.133), kind=kOutput, calls=%fused_computation.91 | convolution fusion | flops 17181966336 | bytes 54525956 | tf_op jit(solution)/shard_map/dot_general | solution.py:25
  1052.6 28.1 %convolution_add_fusion = f32[512,4096]{1,0:T(8,128)} fusion(f32[512,4096]{1,0:T(8,128)} %collective-permute-done.7, bf16[4096,4096]{1,0:T(8,128)(2,1)} %get-tuple-element.72, bf16[4096,2048]{1,0:T(8,128)(2,1)} %fusion.50, s32[]{:T(128)S(6)} %select_n.134), kind=kOutput, calls=%fused_computation.90 | convolution fusion | flops 17181966336 | bytes 54525956 | tf_op jit(solution)/shard_map/dot_general | solution.py:25
  1080.7 45.2 %fusion.38 = f32[2048,2048]{1,0:T(8,128)} fusion(bf16[2048,4096]{1,0:T(8,128)(2,1)} %all-gather.9.cloned.1.call-done, bf16[4096,4096]{1,0:T(8,128)(2,1)} %get-tuple-element.72, s32[]{:T(128)S(6)} %select_n.119), kind=kOutput, calls=%fused_computation.55 | convolution fusion | flops 34359738368 | bytes 50331652 | tf_op jit(solution)/shard_map/dot_general | solution.py:25
  1149.9 52.4 %fusion.15 = (bf16[2048,4096]{1,0:T(8,128)(2,1)}, bf16[2048,4096]{1,0:T(8,128)(2,1)}) fusion(f32[4096]{0:T(1024)S(1)} %bitcast.67, bf16[2048,4096]{1,0:T(8,128)(2,1)} %all-gather.13.cloned.1.call-done, bf16[4096,2048]{1,0:T(8,128)(2,1)} %fusion.50, s32[]{:T(128)S(6)} %select_n.119), kind=kOutput, calls=%fused_computation.25 | convolution fusion | flops 34460401664 | bytes 58736644 | tf_op jit(solution)/shard_map/dot_general | solution.py:25
  1202.3 29.4 %add_convert_fusion.4 = bf16[2048,1024]{1,0:T(8,128)(2,1)} fusion(f32[2048,1024]{1,0:T(8,128)} %fusion.36, f32[1024]{0:T(1024)S(1)} %bitcast.68, bf16[4096,1024]{1,0:T(8,128)(2,1)} %collective-permute-done, s32[]{:T(128)S(6)} %select_n.119, bf16[8192,1024]{1,0:T(8,128)(2,1)} %all-gather.15.cloned.1.call-done, s32[]{:T(128)S(6)} %select_n.121, ...), kind=kOutput, calls=%fused_computation.78 | convolution fusion | flops 17274241024 | bytes 41947144 | tf_op jit(solution)/shard_map/dot_general | solution.py:25
  1231.7 45.9 %fusion.19 = bf16[2048,4096]{1,0:T(8,128)(2,1)} fusion(bf16[2048,4096]{1,0:T(8,128)(2,1)} %get-tuple-element.135, f32[2048,4096]{1,0:T(8,128)} %fusion.62, bf16[8192,1024]{1,0:T(8,128)(2,1)} %all-gather.15.cloned.1.call-done, s32[]{:T(128)S(6)} %select_n.121, bf16[4096,1024]{1,0:T(8,128)(2,1)} %collective-permute-done.1, s32[]{:T(128)S(6)} %select_n.119), kind=kOutput, calls=%fused_computation.29 | convolution fusion | flops 17339252736 | bytes 79691784 | tf_op jit(solution)/shard_map/dot_general | solution.py:25
  1277.7 25.1 %slice_add_fusion = f32[1024,2048]{1,0:T(8,128)} fusion(f32[2048,2048]{1,0:T(8,128)} %fusion.38, bf16[2048,4096]{1,0:T(8,128)(2,1)} %all-gather.13.cloned.1.call-done, bf16[2048,4096]{1,0:T(8,128)(2,1)} %fusion.19), kind=kOutput, calls=%fused_computation.70 | convolution fusion | flops 17181966336 | bytes 41943040 | tf_op jit(solution)/shard_map/dot_general | solution.py:25
  1312.6 24.8 %slice_add_fusion.1 = f32[1024,2048]{1,0:T(8,128)} fusion(f32[2048,2048]{1,0:T(8,128)} %fusion.38, bf16[2048,4096]{1,0:T(8,128)(2,1)} %all-gather.13.cloned.1.call-done, bf16[2048,4096]{1,0:T(8,128)(2,1)} %fusion.19), kind=kOutput, calls=%fused_computation.71 | convolution fusion | flops 17181966336 | bytes 41943040 | tf_op jit(solution)/shard_map/dot_general | solution.py:25
  1348.3 24.5 %add_convert_fusion.3 = bf16[2048,1024]{1,0:T(8,128)(2,1)} fusion(f32[2048,1024]{1,0:T(8,128)} %fusion.46, f32[1024]{0:T(1024)S(1)} %copy-done.21, bf16[4096,1024]{1,0:T(8,128)(2,1)S(1)} %copy-done, s32[]{:T(128)S(6)} %select_n.119, bf16[2048,4096]{1,0:T(8,128)(2,1)} %get-tuple-element.82, bf16[8192,1024]{1,0:T(8,128)(2,1)} %all-gather.7.cloned.1.call-done, ...), kind=kOutput, calls=%fused_computation.73 | convolution fusion | flops 17190354944 | bytes 41947144 | tf_op jit(solution)/shard_map/dot_general | solution.py:25
  1434.8 123.5 %collective-permute-done.13 = f32[2048]{0:T(1024)S(1)} collective-permute-done((f32[2048]{0:T(1024)S(1)}, f32[2048]{0:T(1024)S(1)}, u32[]{:S(2)}, u32[]{:S(2)}) %collective-permute-start.13) | collective-permute-done | bytes 8224 | tf_op jit(solution)/shard_map/ppermute | solution.py:55
  (176 shorter events, 314.9 us)
Async XLA Ops:
  16.0 222.6 %all-gather.9.cloned.1.call-start = ((), (), s32[]{:S(2)}) async-start(), calls=%async_computation.1 | async-start | bytes 25165824 | tf_op jit(solution)/shard_map/all_gather | solution.py:95
  20.4 183.7 %collective-permute-start = (bf16[4096,1024]{1,0:T(8,128)(2,1)}, bf16[4096,1024]{1,0:T(8,128)(2,1)}, u32[]{:S(2)}, u32[]{:S(2)}) collective-permute-start(bf16[4096,1024]{1,0:T(8,128)(2,1)} %param.8), channel_id=1, source_target_pairs={{0,2},{2,0},{1,3},{3,1},{4,6},{6,4},{5,7},{7,5}} | collective-permute-start | bytes 25165832 | tf_op jit(solution)/shard_map/ppermute | solution.py:55
  22.7 523.9 %all-gather.11.cloned.1.call-start = ((), (), s32[]{:S(2)}) async-start(), calls=%async_computation.2 | async-start | bytes 10485760 | tf_op jit(solution)/shard_map/all_gather | solution.py:96
  40.1 322.7 %collective-permute-start.4 = (bf16[1024,1024]{1,0:T(8,128)(2,1)}, bf16[1024,1024]{1,0:T(8,128)(2,1)}, u32[]{:S(2)}, u32[]{:S(2)}) collective-permute-start(bf16[1024,1024]{1,0:T(8,128)(2,1)} %dynamic-slice_select_fusion), channel_id=1, source_target_pairs={{0,2},{2,0},{1,3},{3,1},{4,6},{6,4},{5,7},{7,5}} | collective-permute-start | bytes 6291464 | tf_op jit(solution)/shard_map/ppermute | solution.py:55
  362.8 787.1 %all-gather.13.cloned.1.call-start = ((), (), s32[]{:S(2)}) async-start(), calls=%async_computation.3 | async-start | bytes 25165824 | tf_op jit(solution)/shard_map/all_gather | solution.py:98
  362.9 183.7 %collective-permute-start.1 = (bf16[4096,1024]{1,0:T(8,128)(2,1)}, bf16[4096,1024]{1,0:T(8,128)(2,1)}, u32[]{:S(2)}, u32[]{:S(2)}) collective-permute-start(bf16[4096,1024]{1,0:T(8,128)(2,1)} %param.15), channel_id=1, source_target_pairs={{0,2},{2,0},{1,3},{3,1},{4,6},{6,4},{5,7},{7,5}} | collective-permute-start | bytes 25165832 | tf_op jit(solution)/shard_map/ppermute | solution.py:55
  364.7 361.2 %collective-permute-start.8 = (bf16[1024,4096]{1,0:T(8,128)(2,1)}, bf16[1024,4096]{1,0:T(8,128)(2,1)}, u32[]{:S(2)}, u32[]{:S(2)}) collective-permute-start(bf16[1024,4096]{1,0:T(8,128)(2,1)} %param.11), channel_id=1, source_target_pairs={{0,2},{2,0},{1,3},{3,1},{4,6},{6,4},{5,7},{7,5}} | collective-permute-start | bytes 25165832 | tf_op jit(solution)/shard_map/ppermute | solution.py:55
  657.1 110.9 %collective-permute-start.5 = (f32[2048,1024]{1,0:T(8,128)}, f32[2048,1024]{1,0:T(8,128)}, u32[]{:S(2)}, u32[]{:S(2)}) collective-permute-start(f32[2048,1024]{1,0:T(8,128)} %fusion.42), channel_id=1, source_target_pairs={{0,1},{1,0},{2,3},{3,2},{4,5},{5,4},{6,7},{7,6}} | collective-permute-start | bytes 25165832 | tf_op jit(solution)/shard_map/ppermute | solution.py:55
  725.9 476.4 %all-gather.15.cloned.1.call-start = ((), (), s32[]{:S(2)}) async-start(), calls=%async_computation.4 | async-start | bytes 25165824 | tf_op jit(solution)/shard_map/all_gather | solution.py:97
  726.0 142.1 %collective-permute-start.9 = (bf16[4096,1024]{1,0:T(8,128)(2,1)}, bf16[4096,1024]{1,0:T(8,128)(2,1)}, u32[]{:S(2)}, u32[]{:S(2)}) collective-permute-start(bf16[4096,1024]{1,0:T(8,128)(2,1)} %param.13), channel_id=1, source_target_pairs={{0,2},{3,1},{4,6},{7,5}} | collective-permute-start | bytes 25165832 | tf_op jit(solution)/shard_map/ppermute | solution.py:55
  761.8 242.5 %collective-permute-start.6 = (f32[512,4096]{1,0:T(8,128)}, f32[512,4096]{1,0:T(8,128)}, u32[]{:S(2)}, u32[]{:S(2)}) collective-permute-start(f32[512,4096]{1,0:T(8,128)} %fusion.82), channel_id=1, source_target_pairs={{0,1},{1,0},{2,3},{3,2},{4,5},{5,4},{6,7},{7,6}} | collective-permute-start | bytes 25165832 | tf_op jit(solution)/shard_map/ppermute | solution.py:55
  818.4 232.3 %collective-permute-start.7 = (f32[512,4096]{1,0:T(8,128)}, f32[512,4096]{1,0:T(8,128)}, u32[]{:S(2)}, u32[]{:S(2)}) collective-permute-start(f32[512,4096]{1,0:T(8,128)} %fusion.80), channel_id=1, source_target_pairs={{0,1},{1,0},{2,3},{3,2},{4,5},{5,4},{6,7},{7,6}} | collective-permute-start | bytes 25165832 | tf_op jit(solution)/shard_map/ppermute | solution.py:55
  820.8 175.1 %collective-permute-start.18 = (f32[1024,1024]{1,0:T(8,128)}, f32[1024,1024]{1,0:T(8,128)}, u32[]{:S(2)}, u32[]{:S(2)}) collective-permute-start(f32[1024,1024]{1,0:T(8,128)} %constant_dynamic-slice_fusion.3), channel_id=1, source_target_pairs={{0,4},{4,0},{1,5},{5,1},{2,6},{6,2},{3,7},{7,3}} | collective-permute-start | bytes 12582920 | tf_op jit(solution)/shard_map/ppermute | solution.py:55
  865.8 128.8 %collective-permute-start.15 = (bf16[1024,1024]{1,0:T(8,128)(2,1)}, bf16[1024,1024]{1,0:T(8,128)(2,1)}, u32[]{:S(2)}, u32[]{:S(2)}) collective-permute-start(bf16[1024,1024]{1,0:T(8,128)(2,1)} %add_convert_fusion.6), channel_id=1, source_target_pairs={{0,4},{4,0},{1,5},{5,1},{2,6},{6,2},{3,7},{7,3}} | collective-permute-start | bytes 6291464 | tf_op jit(solution)/shard_map/ppermute | solution.py:55
  869.4 517.2 %collective-permute-start.16 = (bf16[1024,1024]{1,0:T(8,128)(2,1)}, bf16[1024,1024]{1,0:T(8,128)(2,1)}, u32[]{:S(2)}, u32[]{:S(2)}) collective-permute-start(bf16[1024,1024]{1,0:T(8,128)(2,1)} %add_convert_fusion.6), channel_id=1, source_target_pairs={{1,0},{2,3},{5,4},{6,7}} | collective-permute-start | bytes 6291464 | tf_op jit(solution)/shard_map/ppermute | solution.py:55
  994.6 401.7 %collective-permute-start.17 = (bf16[1024,1024]{1,0:T(8,128)(2,1)}, bf16[1024,1024]{1,0:T(8,128)(2,1)}, u32[]{:S(2)}, u32[]{:S(2)}) collective-permute-start(bf16[1024,1024]{1,0:T(8,128)(2,1)} %collective-permute-done.15), channel_id=1, source_target_pairs={{1,0},{2,3},{5,4},{6,7}} | collective-permute-start | bytes 6291464 | tf_op jit(solution)/shard_map/ppermute | solution.py:55
  1046.7 326.2 %collective-permute-start.23 = (f32[512,4096]{1,0:T(8,128)}, f32[512,4096]{1,0:T(8,128)}, u32[]{:S(2)}, u32[]{:S(2)}) collective-permute-start(f32[512,4096]{1,0:T(8,128)} %convolution_add_fusion.1), channel_id=1, source_target_pairs={{0,4},{4,0},{1,5},{5,1},{2,6},{6,2},{3,7},{7,3}} | collective-permute-start | bytes 25165832 | tf_op jit(solution)/shard_map/ppermute | solution.py:55
  1048.7 347.7 %collective-permute-start.21 = (bf16[1024,1024]{1,0:T(8,128)(2,1)}, bf16[1024,1024]{1,0:T(8,128)(2,1)}, u32[]{:S(2)}, u32[]{:S(2)}) collective-permute-start(bf16[1024,1024]{1,0:T(8,128)(2,1)} %collective-permute-done.19), channel_id=1, source_target_pairs={{1,5},{5,1},{2,6},{6,2}} | collective-permute-start | bytes 6291464 | tf_op jit(solution)/shard_map/ppermute | solution.py:55
  1050.6 347.7 %collective-permute-start.22 = (bf16[1024,1024]{1,0:T(8,128)(2,1)}, bf16[1024,1024]{1,0:T(8,128)(2,1)}, u32[]{:S(2)}, u32[]{:S(2)}) collective-permute-start(bf16[1024,1024]{1,0:T(8,128)(2,1)} %collective-permute-done.20), channel_id=1, source_target_pairs={{1,5},{5,1},{2,6},{6,2}} | collective-permute-start | bytes 6291464 | tf_op jit(solution)/shard_map/ppermute | solution.py:55
  1372.9 185.5 %collective-permute-start.10 = (bf16[2048,1024]{1,0:T(8,128)(2,1)}, bf16[2048,1024]{1,0:T(8,128)(2,1)}, u32[]{:S(2)}, u32[]{:S(2)}) collective-permute-start(bf16[2048,1024]{1,0:T(8,128)(2,1)} %add_convert_fusion.4), channel_id=1, source_target_pairs={{0,2},{2,0},{1,3},{3,1},{4,6},{6,4},{5,7},{7,5}} | collective-permute-start | bytes 12582920 | tf_op jit(solution)/shard_map/ppermute | solution.py:55
  1386.6 193.0 %collective-permute-start.24 = (bf16[512,4096]{1,0:T(8,128)(2,1)}, bf16[512,4096]{1,0:T(8,128)(2,1)}, u32[]{:S(2)}, u32[]{:S(2)}) collective-permute-start(bf16[512,4096]{1,0:T(8,128)(2,1)} %add_convert_fusion.2), channel_id=1, source_target_pairs={{0,4},{4,0},{1,5},{5,1},{2,6},{6,2},{3,7},{7,3}} | collective-permute-start | bytes 12582920 | tf_op jit(solution)/shard_map/ppermute | solution.py:55
  1396.3 179.6 %collective-permute-start.11 = (bf16[1024,1024]{1,0:T(8,128)(2,1)S(1)}, bf16[1024,1024]{1,0:T(8,128)(2,1)}, u32[]{:S(2)}, u32[]{:S(2)}) collective-permute-start(bf16[1024,1024]{1,0:T(8,128)(2,1)S(1)} %add_convert_fusion.10), channel_id=1, source_target_pairs={{0,2},{2,0},{1,3},{3,1},{4,6},{6,4},{5,7},{7,5}} | collective-permute-start | bytes 6291464 | tf_op jit(solution)/shard_map/ppermute | solution.py:55
  1396.3 187.9 %collective-permute-start.12 = (bf16[1024,1024]{1,0:T(8,128)(2,1)}, bf16[1024,1024]{1,0:T(8,128)(2,1)}, u32[]{:S(2)}, u32[]{:S(2)}) collective-permute-start(bf16[1024,1024]{1,0:T(8,128)(2,1)} %add_convert_fusion.9), channel_id=1, source_target_pairs={{0,2},{2,0},{1,3},{3,1},{4,6},{6,4},{5,7},{7,5}} | collective-permute-start | bytes 6291464 | tf_op jit(solution)/shard_map/ppermute | solution.py:55
  1398.4 160.0 %collective-permute-start.13 = (f32[2048]{0:T(1024)S(1)}, f32[2048]{0:T(1024)S(1)}, u32[]{:S(2)}, u32[]{:S(2)}) collective-permute-start(f32[2048]{0:T(1024)S(1)} %pad_maximum_fusion.2), channel_id=1, source_target_pairs={{0,2},{2,0},{1,3},{3,1},{4,6},{6,4},{5,7},{7,5}} | collective-permute-start | bytes 24584 | tf_op jit(solution)/shard_map/ppermute | solution.py:55
  (33 other events, 1193.4 us)
Sparse Core Ops, SparseCore 0:
  16.1 28.8 all-gather.6
  46.5 28.4 all-gather.8
  726.1 28.4 all-gather.12
  868.3 26.3 all-gather.14
Sparse Core Ops, SparseCore 1:
  362.9 56.7 all-gather.10
